TPU v7x, 32 devices: a whole 2x2x4 slice. The times are simulated.
32 devices in a mesh: vblk: 4 (over y, x), samp: 8 (over z, core).
Axes of the slice: x: 2, y: 2, z: 4, core: 2. Of those that a mesh axis runs over, the one named last changes fastest.
Arguments:
- vectors: bfloat16 [1024, 32768], P('vblk', 'samp'), may hold values from 0 to 2, as said below
- partner: bfloat16 [1024, 32768], P('vblk', 'samp'), may hold values from 0 to 2, as said below
- next_rows: bfloat16 [1024, 32768], P(('vblk', 'samp')), may hold values from 0 to 2, as said below
Outputs:
- metric: float32 [1024, 256], P('vblk', 'samp')
- next_block: bfloat16 [1024, 32768], P('vblk', 'samp')
Inputs may be any that keep to these rules, and one draw needn't show every extreme that they name: vectors: real expected allele dosages, every entry positive. partner: real expected allele dosages, every entry positive. next_rows: real expected allele dosages, every entry positive.
All inputs are finite; a program needn't handle non-finite values.
Results may differ from a plain program's by a relative error of at most 0.0004.
Values may be sent and summed in bfloat16 or wider, within the bound.
A program may use at most 64 MiB of HBM per device.

v0:
```python
import functools

import jax
import jax.numpy as jnp
from jax import lax
from jax.experimental import pallas as pl
from jax.experimental.pallas import tpu as pltpu
from jax.sharding import PartitionSpec as P

MESH = pl.DeviceIdType.MESH
SUB = 8
ALIGN = 16
WIDTH = 256
UNROLL = 8
TREE = 8
KTILE = 256
ROWS_PER_DOT = 256
VMEM_BYTES = 60 * 1024 * 1024


def from_behind(value, axis, steps):
    count = lax.axis_size(axis)
    pairs = [(source, (source + steps) % count) for source in range(count)]
    return lax.ppermute(value, axis, pairs)


def pair_terms(row_block, col_block):
    row_count = row_block.shape[0]
    grouped = row_block.reshape(row_count // 8, 8, row_block.shape[1])

    def group_sums(row_group):
        return jnp.sum(
            jnp.minimum(row_group[:, None, :], col_block[None, :, :]), axis=2, dtype=jnp.float32
        )

    numerators = lax.map(group_sums, grouped).reshape(row_count, col_block.shape[0])
    row_totals = jnp.sum(row_block, axis=1, dtype=jnp.float32)[:, None]
    col_totals = jnp.sum(col_block, axis=1, dtype=jnp.float32)[None, :]
    return (numerators, row_totals, col_totals)


def plain_body(vectors, partner, next_rows):
    next_block = lax.all_to_all(next_rows, "samp", split_axis=1, concat_axis=0, tiled=True)
    arrived = from_behind(partner, "vblk", 1)
    numerators, row_totals, col_totals = pair_terms(vectors, arrived)
    numerators, col_totals = (
        lax.psum_scatter(numerators, "samp", scatter_dimension=1, tiled=True),
        lax.psum_scatter(col_totals, "samp", scatter_dimension=1, tiled=True),
    )
    row_totals = lax.psum(row_totals, "samp")
    metric = 2.0 * numerators / (row_totals + col_totals)
    return (metric, next_block)


def flipped(index, mask, count):
    out = 0
    bit = 1
    while bit < count:
        out = out + lax.rem(lax.div(index, bit) + lax.div(mask, bit), 2) * bit
        bit *= 2
    return out


def tree_sum(values):
    while len(values) > 1:
        values = [values[i] + values[i + 1] for i in range(0, len(values), 2)]
    return values[0]


def row_sums(block):
    ones = jnp.ones((8, block.shape[1]), jnp.bfloat16)
    return lax.dot_general(
        ones, block, (((1,), (1,)), ((), ())), preferred_element_type=jnp.float32
    )


def kernel(
    n_vblk, n_samp,
    vec_hbm, partner_hbm, next_hbm,
    total_ref, block_hbm,
    vec, wide, arrived, own_piece, part, part_in,
    vec_sem, piece_sem, pair_send, pair_recv, next_send, next_recv, part_send, part_recv,
):
    b = lax.axis_index("vblk")
    s = lax.axis_index("samp")
    up = lax.rem(b + 1, n_vblk)
    down = lax.rem(b + n_vblk - 1, n_vblk)
    row_count, samples = vec.shape
    cols = row_count // n_samp
    next_count = next_hbm.shape[0]
    group = ROWS_PER_DOT // cols
    span = samples // TREE

    vec_copy = pltpu.make_async_copy(vec_hbm, vec, vec_sem)
    vec_copy.start()
    own_in = pltpu.make_async_copy(
        next_hbm.at[:, pl.ds(pl.multiple_of(s * samples, samples), samples)],
        own_piece, piece_sem.at[0],
    )
    own_in.start()

    barrier = pltpu.get_barrier_semaphore()
    for neighbour in (up, down):
        pl.semaphore_signal(barrier, inc=1, device_id=(neighbour, s), device_id_type=MESH)
    for m in range(1, n_samp):
        pl.semaphore_signal(
            barrier, inc=1, device_id=(b, flipped(s, m, n_samp)), device_id_type=MESH
        )
    pl.semaphore_wait(barrier, n_samp + 1)

    def pair_copy(i):
        owner = flipped(s, n_samp - 1 - i, n_samp)
        return pltpu.make_async_remote_copy(
            src_ref=partner_hbm.at[pl.ds(pl.multiple_of(owner * cols, cols), cols), :],
            dst_ref=arrived.at[i],
            send_sem=pair_send.at[i], recv_sem=pair_recv.at[i],
            device_id=(up, s), device_id_type=MESH,
        )

    def next_copy(m):
        peer = flipped(s, m, n_samp)
        return pltpu.make_async_remote_copy(
            src_ref=next_hbm.at[:, pl.ds(pl.multiple_of(peer * samples, samples), samples)],
            dst_ref=block_hbm.at[pl.ds(pl.multiple_of(s * next_count, next_count), next_count), :],
            send_sem=next_send.at[m], recv_sem=next_recv.at[m],
            device_id=(b, peer), device_id_type=MESH,
        )

    def part_copy(i):
        peer = flipped(s, n_samp - 1 - i, n_samp)
        return pltpu.make_async_remote_copy(
            src_ref=part.at[i], dst_ref=part_in.at[i],
            send_sem=part_send.at[i], recv_sem=part_recv.at[i],
            device_id=(b, peer), device_id_type=MESH,
        )

    for i in range(n_samp):
        pair_copy(i).start()
    for m in range(1, n_samp):
        next_copy(m).start()

    own_in.wait()
    own_out = pltpu.make_async_copy(
        own_piece,
        block_hbm.at[pl.ds(pl.multiple_of(s * next_count, next_count), next_count), :],
        piece_sem.at[1],
    )
    own_out.start()

    vec_copy.wait()

    def widen(t, carry):
        first = pl.multiple_of(t * ALIGN, ALIGN)
        for c in range(samples // WIDTH):
            lanes = pl.ds(c * WIDTH, WIDTH)
            rows = vec[pl.ds(first, ALIGN), lanes].astype(jnp.float32)
            for r in range(ALIGN):
                wide[first + r, :, lanes] = jnp.broadcast_to(
                    rows[r:r + 1, :], (SUB, WIDTH)
                ).astype(jnp.bfloat16)
        return carry

    lax.fori_loop(0, row_count // ALIGN, widen, 0)

    own_totals = row_sums(vec[:, pl.ds(0, KTILE)])
    own_totals = lax.fori_loop(
        1, samples // KTILE,
        lambda k, acc: acc + row_sums(vec[:, pl.ds(pl.multiple_of(k * KTILE, KTILE), KTILE)]),
        own_totals,
    )

    groups = row_count // group

    def chunk(i, carry):
        pair_copy(i).wait_recv()

        def one_group(q):
            out = None
            for kt in range(span // KTILE):
                at = [pl.ds((kt * TREE + g) * KTILE, KTILE) for g in range(TREE)]
                pieces = {}
                for half in range(2):
                    js = range(half * cols // SUB // 2, (half + 1) * cols // SUB // 2)
                    theirs = {j: [arrived[i, pl.ds(j * SUB, SUB), o] for o in at] for j in js}
                    for r in range(group):
                        mine = [wide[r * groups + q, :, o] for o in at]
                        for j in js:
                            pieces[r, j] = tree_sum(
                                [jnp.minimum(x, y) for x, y in zip(mine, theirs[j])]
                            )
                minima = jnp.stack([pieces[key] for key in sorted(pieces)])
                sums = row_sums(minima.reshape(ROWS_PER_DOT, KTILE))
                out = sums if out is None else out + sums
            part[i, pl.ds(q, 1), :] = out[0:1, :]

        def groups_step(q, c):
            for k in range(UNROLL):
                one_group(q * UNROLL + k)
            return c

        lax.fori_loop(0, groups // UNROLL, groups_step, 0)
        part[i, pl.ds(groups, 8), :] = own_totals
        part[i, pl.ds(groups + 1, 1), pl.ds(0, cols)] = row_sums(arrived[i])[0:1, :]

        @pl.when(i < n_samp - 1)
        def _():
            part_copy(i).start()

        return carry

    lax.fori_loop(0, n_samp, chunk, 0)

    total = part[n_samp - 1]
    for i in range(n_samp - 1):
        part_copy(i).wait_recv()
        total = total + part_in[i]
    total_ref[...] = total

    for i in range(n_samp):
        pair_copy(i).wait_send()
    for i in range(n_samp - 1):
        part_copy(i).wait_send()
    for m in range(1, n_samp):
        next_copy(m).wait()
    own_out.wait()


def finish(
    groups, cols, total_hbm, block_in, metric_hbm, block_out,
    total_ref, metric_ref, pieces, in_sems, out_sems, end_sems,
):
    count, rows, _ = pieces.shape

    def take(i):
        return pltpu.make_async_copy(
            block_in.at[pl.ds(i * rows, rows), :], pieces.at[i], in_sems.at[i]
        )

    def give(i):
        return pltpu.make_async_copy(
            pieces.at[i], block_out.at[pl.ds(i * rows, rows), :], out_sems.at[i]
        )

    total_in = pltpu.make_async_copy(total_hbm, total_ref, end_sems.at[0])
    metric_out = pltpu.make_async_copy(metric_ref, metric_hbm, end_sems.at[1])
    total_in.start()
    for i in range(count):
        take(i).start()
    total_in.wait()
    turned = total_ref[pl.ds(0, groups), :].T
    numerators = jnp.concatenate(
        [turned[first:first + cols, :] for first in range(0, turned.shape[0], cols)], axis=1
    )
    own_totals = total_ref[pl.ds(groups, 1), :]
    pair_totals = total_ref[pl.ds(groups, 8), :].T[:cols, 1:2]
    metric_ref[...] = 2.0 * numerators / (own_totals + pair_totals)
    metric_out.start()
    for i in range(count):
        take(i).wait()
        give(i).start()
    for i in range(count):
        give(i).wait()
    metric_out.wait()


def fused_body(n_vblk, n_samp, vectors, partner, next_rows):
    rows, samples = vectors.shape
    cols = rows // n_samp
    groups = rows * cols // ROWS_PER_DOT
    part_rows = groups + 8
    next_count = next_rows.shape[0]
    hbm = pl.BlockSpec(memory_space=pl.ANY)
    dma = pltpu.SemaphoreType.DMA
    total, next_block = pl.pallas_call(
        functools.partial(kernel, n_vblk, n_samp),
        out_shape=(
            jax.ShapeDtypeStruct((part_rows, ROWS_PER_DOT), jnp.float32),
            jax.ShapeDtypeStruct((next_count * n_samp, samples), next_rows.dtype),
        ),
        in_specs=[hbm, hbm, hbm],
        out_specs=(pl.BlockSpec(memory_space=pltpu.VMEM), hbm),
        scratch_shapes=[
            pltpu.VMEM((rows, samples), jnp.bfloat16),
            pltpu.VMEM((rows, SUB, samples), jnp.bfloat16),
            pltpu.VMEM((n_samp, cols, samples), jnp.bfloat16),
            pltpu.VMEM((next_count, samples), jnp.bfloat16),
            pltpu.VMEM((n_samp, part_rows, ROWS_PER_DOT), jnp.float32),
            pltpu.VMEM((n_samp - 1, part_rows, ROWS_PER_DOT), jnp.float32),
            dma, dma((2,)),
            dma((n_samp,)), dma((n_samp,)),
            dma((n_samp,)), dma((n_samp,)),
            dma((n_samp,)), dma((n_samp,)),
        ],
        compiler_params=pltpu.CompilerParams(
            collective_id=0, has_side_effects=True, vmem_limit_bytes=VMEM_BYTES
        ),
        name="similarity",
    )(vectors, partner, next_rows)
    metric, next_block = pl.pallas_call(
        functools.partial(finish, groups, cols),
        out_shape=(
            jax.ShapeDtypeStruct((cols, rows), jnp.float32),
            jax.ShapeDtypeStruct(next_block.shape, next_block.dtype),
        ),
        in_specs=[hbm, hbm],
        out_specs=(hbm, hbm),
        scratch_shapes=[
            pltpu.VMEM((part_rows, ROWS_PER_DOT), jnp.float32),
            pltpu.VMEM((cols, rows), jnp.float32),
            pltpu.VMEM((n_samp, next_count, samples), next_rows.dtype),
            dma((n_samp,)), dma((n_samp,)), dma((2,)),
        ],
        name="finish",
    )(total, next_block)
    return (metric.T, next_block)


def body(n_vblk, n_samp, vectors, partner, next_rows):
    rows, samples = vectors.shape
    cols = rows // n_samp
    fits = (
        n_vblk > 2
        and n_samp > 1
        and n_samp & (n_samp - 1) == 0
        and rows == ROWS_PER_DOT
        and cols % ALIGN == 0
        and cols % UNROLL == 0
        and samples % (TREE * KTILE) == 0
        and next_rows.shape[0] % ALIGN == 0
        and rows * SUB * samples * 2 + 4 * rows * samples * 2 <= VMEM_BYTES
        and next_rows.shape[0] * n_samp == rows
    )
    if fits:
        return fused_body(n_vblk, n_samp, vectors, partner, next_rows)
    return plain_body(vectors, partner, next_rows)


def solution(mesh):
    in_specs = (P("vblk", "samp"), P("vblk", "samp"), P(("vblk", "samp"), None))
    out_specs = (P("vblk", "samp"), P("vblk", "samp"))
    step = functools.partial(body, mesh.shape["vblk"], mesh.shape["samp"])
    return jax.shard_map(step, mesh=mesh, in_specs=in_specs, out_specs=out_specs, check_vma=False)
```

profile of v0, /device:TPU:1, one launch (start us, length us, event | category | flops | bytes accessed | tf_op | source)
XLA Modules:
  0.0 62.9 jit_solution(16780115533162959348)
XLA Ops:
  0.6 59.2 %similarity.1 = (f32[40,256]{1,0:T(8,128)}, bf16[256,4096]{1,0:T(8,128)(2,1)}) custom-call(bf16[256,4096]{1,0:T(8,128)(2,1)} %vec_hbm.1, bf16[256,4096]{1,0:T(8,128)(2,1)} %partner_hbm.1, bf16[32,32768]{1,0:T(8,128)(2,1)} %next_hbm.1), custom_call_target="tpu_custom_call" | custom-call | tf_op jit(solution)/shard_map/similarity/pallas_call | solution.py:274
  59.9 3.0 %finish.1 = (f32[32,256]{1,0:T(8,128)}, bf16[256,4096]{1,0:T(8,128)(2,1)}) custom-call(f32[40,256]{1,0:T(8,128)} %get-tuple-element.6.total_hbm, bf16[256,4096]{1,0:T(8,128)(2,1)} %get-tuple-element.7.block_in), custom_call_target="tpu_custom_call" | custom-call | tf_op jit(solution)/shard_map/finish/pallas_call | solution.py:299
where the time goes:
time: 64.1 us; the launch traced here: 62.9 us
  Pallas kernels  62.2 us (97%)
    pallas_call x1, Pallas kernels, fused_body(): pl.pallas_call(functools.partial(kernel, n_vblk, n_samp), out_shape=(jax....  59.2 us
    pallas_call x1, Pallas kernels, fused_body(): pl.pallas_call(functools.partial(finish, groups, cols), out_shape=(jax.Sh...  3.04 us

commit v1 on v0

--- a/solution.py
+++ b/solution.py
@@ -74,22 +74,33 @@
     )
 
 
+def spread(slot, count):
+    out = 0
+    bit = 1
+    while bit < count:
+        out = out + lax.rem(lax.div(slot, bit), 2) * (count // (2 * bit))
+        bit *= 2
+    return out
+
+
 def kernel(
     n_vblk, n_samp,
     vec_hbm, partner_hbm, next_hbm,
     total_ref, block_hbm,
     vec, wide, arrived, own_piece, part, part_in,
-    vec_sem, piece_sem, pair_send, pair_recv, next_send, next_recv, part_send, part_recv,
+    vec_sem, piece_sem, go_sem, pair_send, pair_recv, next_send, next_recv, part_send, part_recv,
 ):
     b = lax.axis_index("vblk")
     s = lax.axis_index("samp")
     up = lax.rem(b + 1, n_vblk)
     down = lax.rem(b + n_vblk - 1, n_vblk)
+    odd = lax.rem(s, 2)
     row_count, samples = vec.shape
     cols = row_count // n_samp
     next_count = next_hbm.shape[0]
     group = ROWS_PER_DOT // cols
-    span = samples // TREE
+    span = TREE * KTILE
+    units = samples // span
 
     vec_copy = pltpu.make_async_copy(vec_hbm, vec, vec_sem)
     vec_copy.start()
@@ -100,20 +111,21 @@
     own_in.start()
 
     barrier = pltpu.get_barrier_semaphore()
-    for neighbour in (up, down):
-        pl.semaphore_signal(barrier, inc=1, device_id=(neighbour, s), device_id_type=MESH)
-    for m in range(1, n_samp):
-        pl.semaphore_signal(
-            barrier, inc=1, device_id=(b, flipped(s, m, n_samp)), device_id_type=MESH
-        )
-    pl.semaphore_wait(barrier, n_samp + 1)
-
-    def pair_copy(i):
-        owner = flipped(s, n_samp - 1 - i, n_samp)
+    pl.semaphore_signal(barrier, inc=1, device_id=(down, s), device_id_type=MESH)
+    for peer in range(1, n_samp, 2):
+        @pl.when(s != peer)
+        def _():
+            pl.semaphore_signal(barrier, inc=1, device_id=(b, peer), device_id_type=MESH)
+    pl.semaphore_wait(barrier, 1 + odd * (n_samp - 1))
+
+    def pair_copy(x, u):
+        owner = flipped(s, spread(x, n_samp), n_samp)
         return pltpu.make_async_remote_copy(
-            src_ref=partner_hbm.at[pl.ds(pl.multiple_of(owner * cols, cols), cols), :],
-            dst_ref=arrived.at[i],
-            send_sem=pair_send.at[i], recv_sem=pair_recv.at[i],
+            src_ref=partner_hbm.at[
+                pl.ds(pl.multiple_of(owner * cols, cols), cols), pl.ds(u * span, span)
+            ],
+            dst_ref=arrived.at[x, :, pl.ds(u * span, span)],
+            send_sem=pair_send.at[x * units + u], recv_sem=pair_recv.at[x * units + u],
             device_id=(up, s), device_id_type=MESH,
         )
 
@@ -126,16 +138,25 @@
             device_id=(b, peer), device_id_type=MESH,
         )
 
-    def part_copy(i):
-        peer = flipped(s, n_samp - 1 - i, n_samp)
+    def part_copy(x, mask):
         return pltpu.make_async_remote_copy(
-            src_ref=part.at[i], dst_ref=part_in.at[i],
-            send_sem=part_send.at[i], recv_sem=part_recv.at[i],
-            device_id=(b, peer), device_id_type=MESH,
-        )
-
-    for i in range(n_samp):
-        pair_copy(i).start()
+            src_ref=part.at[x], dst_ref=part_in.at[x],
+            send_sem=part_send.at[x], recv_sem=part_recv.at[x],
+            device_id=(b, flipped(s, mask, n_samp)), device_id_type=MESH,
+        )
+
+    for x in reversed(range(n_samp)):
+        for u in range(units):
+            pair_copy(x, u).start()
+
+    @pl.when(odd == 1)
+    def _():
+        pl.semaphore_signal(go_sem, inc=1, device_id=(b, s - 1), device_id_type=MESH)
+
+    @pl.when(odd == 0)
+    def _():
+        pl.semaphore_wait(go_sem, 1)
+
     for m in range(1, n_samp):
         next_copy(m).start()
 
@@ -172,54 +193,60 @@
     groups = row_count // group
 
     def chunk(i, carry):
-        pair_copy(i).wait_recv()
-
-        def one_group(q):
-            out = None
-            for kt in range(span // KTILE):
-                at = [pl.ds((kt * TREE + g) * KTILE, KTILE) for g in range(TREE)]
+        x = n_samp - 1 - i
+        for u in range(units):
+            pair_copy(x, u).wait_recv()
+            at = [pl.ds(u * span + g * KTILE, KTILE) for g in range(TREE)]
+
+            def one_group(q):
                 pieces = {}
                 for half in range(2):
                     js = range(half * cols // SUB // 2, (half + 1) * cols // SUB // 2)
-                    theirs = {j: [arrived[i, pl.ds(j * SUB, SUB), o] for o in at] for j in js}
+                    theirs = {j: [arrived[x, pl.ds(j * SUB, SUB), o] for o in at] for j in js}
                     for r in range(group):
                         mine = [wide[r * groups + q, :, o] for o in at]
                         for j in js:
                             pieces[r, j] = tree_sum(
-                                [jnp.minimum(x, y) for x, y in zip(mine, theirs[j])]
+                                [jnp.minimum(v, w) for v, w in zip(mine, theirs[j])]
                             )
                 minima = jnp.stack([pieces[key] for key in sorted(pieces)])
-                sums = row_sums(minima.reshape(ROWS_PER_DOT, KTILE))
-                out = sums if out is None else out + sums
-            part[i, pl.ds(q, 1), :] = out[0:1, :]
-
-        def groups_step(q, c):
-            for k in range(UNROLL):
-                one_group(q * UNROLL + k)
-            return c
-
-        lax.fori_loop(0, groups // UNROLL, groups_step, 0)
-        part[i, pl.ds(groups, 8), :] = own_totals
-        part[i, pl.ds(groups + 1, 1), pl.ds(0, cols)] = row_sums(arrived[i])[0:1, :]
-
-        @pl.when(i < n_samp - 1)
-        def _():
-            part_copy(i).start()
-
+                sums = row_sums(minima.reshape(ROWS_PER_DOT, KTILE))[0:1, :]
+                if u:
+                    sums = sums + part[x, pl.ds(q, 1), :]
+                part[x, pl.ds(q, 1), :] = sums
+
+            def groups_step(q, c):
+                for k in range(UNROLL):
+                    one_group(q * UNROLL + k)
+                return c
+
+            lax.fori_loop(0, groups // UNROLL, groups_step, 0)
+        part[x, pl.ds(groups, 8), :] = own_totals
+        part[x, pl.ds(groups + 1, 1), pl.ds(0, cols)] = row_sums(arrived[x])[0:1, :]
+
+        bit = n_samp // 2
+        while bit:
+            @pl.when(x < bit)
+            def _(bit=bit):
+                part_copy(x + bit, n_samp // (2 * bit)).wait_recv()
+                part[x] = part[x] + part_in[x + bit]
+            bit //= 2
+        bit = n_samp // 2
+        while bit:
+            @pl.when((x >= bit) & (x < 2 * bit))
+            def _(bit=bit):
+                part_copy(x, n_samp // (2 * bit)).start()
+            bit //= 2
         return carry
 
     lax.fori_loop(0, n_samp, chunk, 0)
-
-    total = part[n_samp - 1]
-    for i in range(n_samp - 1):
-        part_copy(i).wait_recv()
-        total = total + part_in[i]
-    total_ref[...] = total
-
-    for i in range(n_samp):
-        pair_copy(i).wait_send()
-    for i in range(n_samp - 1):
-        part_copy(i).wait_send()
+    total_ref[...] = part[0]
+
+    for x in range(n_samp):
+        for u in range(units):
+            pair_copy(x, u).wait_send()
+    for x in range(1, n_samp):
+        part_copy(x, 1).wait_send()
     for m in range(1, n_samp):
         next_copy(m).wait()
     own_out.wait()
@@ -267,6 +294,7 @@
     rows, samples = vectors.shape
     cols = rows // n_samp
     groups = rows * cols // ROWS_PER_DOT
+    units = samples // (TREE * KTILE)
     part_rows = groups + 8
     next_count = next_rows.shape[0]
     hbm = pl.BlockSpec(memory_space=pl.ANY)
@@ -285,9 +313,9 @@
             pltpu.VMEM((n_samp, cols, samples), jnp.bfloat16),
             pltpu.VMEM((next_count, samples), jnp.bfloat16),
             pltpu.VMEM((n_samp, part_rows, ROWS_PER_DOT), jnp.float32),
-            pltpu.VMEM((n_samp - 1, part_rows, ROWS_PER_DOT), jnp.float32),
-            dma, dma((2,)),
-            dma((n_samp,)), dma((n_samp,)),
+            pltpu.VMEM((n_samp, part_rows, ROWS_PER_DOT), jnp.float32),
+            dma, dma((2,)), pltpu.SemaphoreType.REGULAR,
+            dma((n_samp * units,)), dma((n_samp * units,)),
             dma((n_samp,)), dma((n_samp,)),
             dma((n_samp,)), dma((n_samp,)),
         ],

time: 64.1 us -> 61.4 us (0.958); the launches traced: 62.9 us -> 61.3 us
  Pallas kernels: 62.2 us -> 60.6 us
    pallas_call x1, Pallas kernels: 59.2 us -> 57.6 us  [fused_body(): pl.pallas_call(functools.partial(kernel, n_vblk, n_samp), out_shape=(jax....]
where the time goes in v1:
time: 61.4 us; the launch traced here: 61.3 us
  Pallas kernels  60.6 us (99%)
  between operations  0.64 us (1%)
    pallas_call x1, Pallas kernels, fused_body(): pl.pallas_call(functools.partial(kernel, n_vblk, n_samp), out_shape=(jax....  57.6 us
    pallas_call x1, Pallas kernels, fused_body(): pl.pallas_call(functools.partial(finish, groups, cols), out_shape=(jax.Sh...  3.04 us

profile of v1, /device:TPU:1, one launch (start us, length us, event | category | flops | bytes accessed | tf_op | source)
XLA Modules:
  0.0 61.3 jit_solution(6523074276987439478)
XLA Ops:
  0.6 57.6 %similarity.1 = (f32[40,256]{1,0:T(8,128)}, bf16[256,4096]{1,0:T(8,128)(2,1)}) custom-call(bf16[256,4096]{1,0:T(8,128)(2,1)} %vec_hbm.1, bf16[256,4096]{1,0:T(8,128)(2,1)} %partner_hbm.1, bf16[32,32768]{1,0:T(8,128)(2,1)} %next_hbm.1), custom_call_target="tpu_custom_call" | custom-call | tf_op jit(solution)/shard_map/similarity/pallas_call | solution.py:302
  58.2 3.0 %finish.1 = (f32[32,256]{1,0:T(8,128)}, bf16[256,4096]{1,0:T(8,128)(2,1)}) custom-call(f32[40,256]{1,0:T(8,128)} %get-tuple-element.6.total_hbm, bf16[256,4096]{1,0:T(8,128)(2,1)} %get-tuple-element.7.block_in), custom_call_target="tpu_custom_call" | custom-call | tf_op jit(solution)/shard_map/finish/pallas_call | solution.py:327

commit v2 on v1

--- a/solution.py
+++ b/solution.py
@@ -11,11 +11,12 @@
 SUB = 8
 ALIGN = 16
 WIDTH = 256
-UNROLL = 8
+UNROLL = 32
 TREE = 8
 KTILE = 256
 ROWS_PER_DOT = 256
 VMEM_BYTES = 60 * 1024 * 1024
+KERNEL_BYTES = 51712 * 1024
 
 
 def from_behind(value, axis, steps):
@@ -253,27 +254,11 @@
 
 
 def finish(
-    groups, cols, total_hbm, block_in, metric_hbm, block_out,
-    total_ref, metric_ref, pieces, in_sems, out_sems, end_sems,
+    groups, cols, total_ref, block_in, metric_hbm, block_out, metric_ref, end_sems,
 ):
-    count, rows, _ = pieces.shape
-
-    def take(i):
-        return pltpu.make_async_copy(
-            block_in.at[pl.ds(i * rows, rows), :], pieces.at[i], in_sems.at[i]
-        )
-
-    def give(i):
-        return pltpu.make_async_copy(
-            pieces.at[i], block_out.at[pl.ds(i * rows, rows), :], out_sems.at[i]
-        )
-
-    total_in = pltpu.make_async_copy(total_hbm, total_ref, end_sems.at[0])
-    metric_out = pltpu.make_async_copy(metric_ref, metric_hbm, end_sems.at[1])
-    total_in.start()
-    for i in range(count):
-        take(i).start()
-    total_in.wait()
+    block_copy = pltpu.make_async_copy(block_in, block_out, end_sems.at[0])
+    metric_copy = pltpu.make_async_copy(metric_ref, metric_hbm, end_sems.at[1])
+    block_copy.start()
     turned = total_ref[pl.ds(0, groups), :].T
     numerators = jnp.concatenate(
         [turned[first:first + cols, :] for first in range(0, turned.shape[0], cols)], axis=1
@@ -281,13 +266,9 @@
     own_totals = total_ref[pl.ds(groups, 1), :]
     pair_totals = total_ref[pl.ds(groups, 8), :].T[:cols, 1:2]
     metric_ref[...] = 2.0 * numerators / (own_totals + pair_totals)
-    metric_out.start()
-    for i in range(count):
-        take(i).wait()
-        give(i).start()
-    for i in range(count):
-        give(i).wait()
-    metric_out.wait()
+    metric_copy.start()
+    block_copy.wait()
+    metric_copy.wait()
 
 
 def fused_body(n_vblk, n_samp, vectors, partner, next_rows):
@@ -305,7 +286,7 @@
             jax.ShapeDtypeStruct((part_rows, ROWS_PER_DOT), jnp.float32),
             jax.ShapeDtypeStruct((next_count * n_samp, samples), next_rows.dtype),
         ),
-        in_specs=[hbm, hbm, hbm],
+        in_specs=[pl.BlockSpec(memory_space=pltpu.HBM)] * 3,
         out_specs=(pl.BlockSpec(memory_space=pltpu.VMEM), hbm),
         scratch_shapes=[
             pltpu.VMEM((rows, samples), jnp.bfloat16),
@@ -320,7 +301,7 @@
             dma((n_samp,)), dma((n_samp,)),
         ],
         compiler_params=pltpu.CompilerParams(
-            collective_id=0, has_side_effects=True, vmem_limit_bytes=VMEM_BYTES
+            collective_id=0, has_side_effects=True, vmem_limit_bytes=KERNEL_BYTES
         ),
         name="similarity",
     )(vectors, partner, next_rows)
@@ -330,14 +311,10 @@
             jax.ShapeDtypeStruct((cols, rows), jnp.float32),
             jax.ShapeDtypeStruct(next_block.shape, next_block.dtype),
         ),
-        in_specs=[hbm, hbm],
+        in_specs=[pl.BlockSpec(memory_space=pltpu.VMEM)] * 2,
         out_specs=(hbm, hbm),
-        scratch_shapes=[
-            pltpu.VMEM((part_rows, ROWS_PER_DOT), jnp.float32),
-            pltpu.VMEM((cols, rows), jnp.float32),
-            pltpu.VMEM((n_samp, next_count, samples), next_rows.dtype),
-            dma((n_samp,)), dma((n_samp,)), dma((2,)),
-        ],
+        scratch_shapes=[pltpu.VMEM((cols, rows), jnp.float32), dma((2,))],
+        compiler_params=pltpu.CompilerParams(vmem_limit_bytes=8 * 1024 * 1024),
         name="finish",
     )(total, next_block)
     return (metric.T, next_block)
@@ -352,7 +329,7 @@
         and n_samp & (n_samp - 1) == 0
         and rows == ROWS_PER_DOT
         and cols % ALIGN == 0
-        and cols % UNROLL == 0
+        and (rows * cols // ROWS_PER_DOT) % UNROLL == 0
         and samples % (TREE * KTILE) == 0
         and next_rows.shape[0] % ALIGN == 0
         and rows * SUB * samples * 2 + 4 * rows * samples * 2 <= VMEM_BYTES

time: 61.4 us -> 57.5 us (0.936)
  Pallas kernels: 60.6 us -> 56.7 us
    pallas_call x1, Pallas kernels: 57.6 us -> 55.3 us  [fused_body(): pl.pallas_call(functools.partial(kernel, n_vblk, n_samp), out_shape=(jax....]
    pallas_call x1, Pallas kernels: 3.04 us -> 1.34 us  [fused_body(): pl.pallas_call(functools.partial(finish, groups, cols), out_shape=(jax.Sh...]
where the time goes in v2:
time: 57.5 us; the launch traced here: 57.3 us
  Pallas kernels  56.7 us (99%)
  between operations  0.64 us (1%)
    pallas_call x1, Pallas kernels, fused_body(): pl.pallas_call(functools.partial(kernel, n_vblk, n_samp), out_shape=(jax....  55.3 us
    pallas_call x1, Pallas kernels, fused_body(): pl.pallas_call(functools.partial(finish, groups, cols), out_shape=(jax.Sh...  1.34 us

profile of v2, /device:TPU:1, one launch (start us, length us, event | category | flops | bytes accessed | tf_op | source)
XLA Modules:
  0.0 57.3 jit_solution(3970711148897246074)
XLA Ops:
  0.6 55.3 %similarity.1 = (f32[40,256]{1,0:T(8,128)S(1)}, bf16[256,4096]{1,0:T(8,128)(2,1)S(1)}) custom-call(bf16[256,4096]{1,0:T(8,128)(2,1)} %vec_hbm.1, bf16[256,4096]{1,0:T(8,128)(2,1)} %partner_hbm.1, bf16[32,32768]{1,0:T(8,128)(2,1)} %next_hbm.1), custom_call_target="tpu_custom_call" | custom-call | tf_op jit(solution)/shard_map/similarity/pallas_call | solution.py:283
  56.0 1.3 %finish.1 = (f32[32,256]{1,0:T(8,128)}, bf16[256,4096]{1,0:T(8,128)(2,1)}) custom-call(f32[40,256]{1,0:T(8,128)S(1)} %get-tuple-element.6.total_ref, bf16[256,4096]{1,0:T(8,128)(2,1)S(1)} %get-tuple-element.7.block_in), custom_call_target="tpu_custom_call" | custom-call | tf_op jit(solution)/shard_map/finish/pallas_call | solution.py:308

commit v3 on v2

--- a/solution.py
+++ b/solution.py
@@ -11,8 +11,8 @@
 SUB = 8
 ALIGN = 16
 WIDTH = 256
-UNROLL = 32
 TREE = 8
+TAIL_TREE = 4
 KTILE = 256
 ROWS_PER_DOT = 256
 VMEM_BYTES = 60 * 1024 * 1024
@@ -68,8 +68,9 @@
     return values[0]
 
 
-def row_sums(block):
-    ones = jnp.ones((8, block.shape[1]), jnp.bfloat16)
+def row_sums(block, ones=None):
+    if ones is None:
+        ones = jnp.ones((SUB, block.shape[1]), jnp.bfloat16)
     return lax.dot_general(
         ones, block, (((1,), (1,)), ((), ())), preferred_element_type=jnp.float32
     )
@@ -100,7 +101,7 @@
     cols = row_count // n_samp
     next_count = next_hbm.shape[0]
     group = ROWS_PER_DOT // cols
-    span = TREE * KTILE
+    span = TAIL_TREE * KTILE
     units = samples // span
 
     vec_copy = pltpu.make_async_copy(vec_hbm, vec, vec_sem)
@@ -146,9 +147,14 @@
             device_id=(b, flipped(s, mask, n_samp)), device_id_type=MESH,
         )
 
-    for x in reversed(range(n_samp)):
-        for u in range(units):
-            pair_copy(x, u).start()
+    def start_pairs(chunks):
+        for x in chunks:
+            for u in range(units):
+                pair_copy(x, u).start()
+
+    held = n_samp // 4
+    start_pairs(reversed(range(held, n_samp)))
+    pl.when(odd == 1)(functools.partial(start_pairs, reversed(range(held))))
 
     @pl.when(odd == 1)
     def _():
@@ -193,54 +199,68 @@
 
     groups = row_count // group
 
+    rows_of = lax.broadcasted_iota(jnp.int32, (SUB, KTILE), 0)
+    one_row = [(rows_of == k).astype(jnp.bfloat16) for k in range(SUB)]
+
+    def add_unit(x, first, tree):
+        for u in range(first // span, (first + tree * KTILE) // span):
+            pair_copy(x, u).wait_recv()
+        at = [pl.ds(first + g * KTILE, KTILE) for g in range(tree)]
+
+        def one_group(q):
+            pieces = {}
+            for half in range(2):
+                js = range(half * cols // SUB // 2, (half + 1) * cols // SUB // 2)
+                theirs = {j: [arrived[x, pl.ds(j * SUB, SUB), o] for o in at] for j in js}
+                for r in range(group):
+                    mine = [wide[r * groups + q, :, o] for o in at]
+                    for j in js:
+                        pieces[r, j] = tree_sum(
+                            [jnp.minimum(v, w) for v, w in zip(mine, theirs[j])]
+                        )
+            minima = jnp.stack(list(pieces.values()))
+            return row_sums(minima.reshape(ROWS_PER_DOT, KTILE), one_row[q % SUB])
+
+        for q in range(0, groups, SUB):
+            sums = one_group(q)
+            for k in range(1, SUB):
+                sums = sums + one_group(q + k)
+            if first:
+                sums = sums + part[x, pl.ds(q, SUB), :]
+            part[x, pl.ds(q, SUB), :] = sums
+
+    def add_totals(x):
+        part[x, pl.ds(groups, 8), :] = own_totals
+        part[x, pl.ds(groups + 1, 1), pl.ds(0, cols)] = row_sums(arrived[x])[0:1, :]
+
+    def add_parts(x, bit):
+        part_copy(x + bit, n_samp // (2 * bit)).wait_recv()
+        part[x] = part[x] + part_in[x + bit]
+
     def chunk(i, carry):
         x = n_samp - 1 - i
-        for u in range(units):
-            pair_copy(x, u).wait_recv()
-            at = [pl.ds(u * span + g * KTILE, KTILE) for g in range(TREE)]
-
-            def one_group(q):
-                pieces = {}
-                for half in range(2):
-                    js = range(half * cols // SUB // 2, (half + 1) * cols // SUB // 2)
-                    theirs = {j: [arrived[x, pl.ds(j * SUB, SUB), o] for o in at] for j in js}
-                    for r in range(group):
-                        mine = [wide[r * groups + q, :, o] for o in at]
-                        for j in js:
-                            pieces[r, j] = tree_sum(
-                                [jnp.minimum(v, w) for v, w in zip(mine, theirs[j])]
-                            )
-                minima = jnp.stack([pieces[key] for key in sorted(pieces)])
-                sums = row_sums(minima.reshape(ROWS_PER_DOT, KTILE))[0:1, :]
-                if u:
-                    sums = sums + part[x, pl.ds(q, 1), :]
-                part[x, pl.ds(q, 1), :] = sums
-
-            def groups_step(q, c):
-                for k in range(UNROLL):
-                    one_group(q * UNROLL + k)
-                return c
-
-            lax.fori_loop(0, groups // UNROLL, groups_step, 0)
-        part[x, pl.ds(groups, 8), :] = own_totals
-        part[x, pl.ds(groups + 1, 1), pl.ds(0, cols)] = row_sums(arrived[x])[0:1, :]
-
-        bit = n_samp // 2
-        while bit:
-            @pl.when(x < bit)
-            def _(bit=bit):
-                part_copy(x + bit, n_samp // (2 * bit)).wait_recv()
-                part[x] = part[x] + part_in[x + bit]
-            bit //= 2
-        bit = n_samp // 2
-        while bit:
+        for first in range(0, samples, TREE * KTILE):
+            add_unit(x, first, TREE)
+        add_totals(x)
+        bits = [n_samp >> k for k in range(1, n_samp.bit_length())]
+        for bit in bits:
+            pl.when(x < bit)(functools.partial(add_parts, x, bit))
+        for bit in bits:
             @pl.when((x >= bit) & (x < 2 * bit))
             def _(bit=bit):
                 part_copy(x, n_samp // (2 * bit)).start()
-            bit //= 2
+        pl.when((i == n_samp // 2) & (odd == 0))(functools.partial(start_pairs, reversed(range(held))))
         return carry
 
-    lax.fori_loop(0, n_samp, chunk, 0)
+    lax.fori_loop(0, n_samp - 1, chunk, 0)
+
+    for first in range(0, samples - TREE * KTILE, TREE * KTILE):
+        add_unit(0, first, TREE)
+    for first in range(samples - TREE * KTILE, samples, TAIL_TREE * KTILE):
+        add_unit(0, first, TAIL_TREE)
+    add_totals(0)
+    for k in range(1, n_samp.bit_length()):
+        add_parts(0, n_samp >> k)
     total_ref[...] = part[0]
 
     for x in range(n_samp):
@@ -260,8 +280,16 @@
     metric_copy = pltpu.make_async_copy(metric_ref, metric_hbm, end_sems.at[1])
     block_copy.start()
     turned = total_ref[pl.ds(0, groups), :].T
+    half = cols // 2
     numerators = jnp.concatenate(
-        [turned[first:first + cols, :] for first in range(0, turned.shape[0], cols)], axis=1
+        [
+            jnp.concatenate(
+                [turned[part + first:part + first + half, :] for part in (0, turned.shape[0] // 2)],
+                axis=0,
+            )
+            for first in range(0, turned.shape[0] // 2, half)
+        ],
+        axis=1,
     )
     own_totals = total_ref[pl.ds(groups, 1), :]
     pair_totals = total_ref[pl.ds(groups, 8), :].T[:cols, 1:2]
@@ -275,7 +303,7 @@
     rows, samples = vectors.shape
     cols = rows // n_samp
     groups = rows * cols // ROWS_PER_DOT
-    units = samples // (TREE * KTILE)
+    units = samples // (TAIL_TREE * KTILE)
     part_rows = groups + 8
     next_count = next_rows.shape[0]
     hbm = pl.BlockSpec(memory_space=pl.ANY)
@@ -329,7 +357,6 @@
         and n_samp & (n_samp - 1) == 0
         and rows == ROWS_PER_DOT
         and cols % ALIGN == 0
-        and (rows * cols // ROWS_PER_DOT) % UNROLL == 0
         and samples % (TREE * KTILE) == 0
         and next_rows.shape[0] % ALIGN == 0
         and rows * SUB * samples * 2 + 4 * rows * samples * 2 <= VMEM_BYTES

time: 57.5 us -> 56.9 us (0.990)
  Pallas kernels: 56.7 us -> 55.7 us
    pallas_call x1, Pallas kernels: 55.3 us -> 54.3 us  [fused_body(): pl.pallas_call(functools.partial(kernel, n_vblk, n_samp), out_shape=(jax....]
where the time goes in v3:
time: 56.9 us; the launch traced here: 56.3 us
  Pallas kernels  55.7 us (98%)
  between operations  0.64 us (1%)
    pallas_call x1, Pallas kernels, fused_body(): pl.pallas_call(functools.partial(kernel, n_vblk, n_samp), out_shape=(jax....  54.3 us
    pallas_call x1, Pallas kernels, fused_body(): pl.pallas_call(functools.partial(finish, groups, cols), out_shape=(jax.Sh...  1.34 us

profile of v3, /device:TPU:1, one launch (start us, length us, event | category | flops | bytes accessed | tf_op | source)
XLA Modules:
  0.0 56.3 jit_solution(6380282385024127754)
XLA Ops:
  0.6 54.3 %similarity.1 = (f32[40,256]{1,0:T(8,128)S(1)}, bf16[256,4096]{1,0:T(8,128)(2,1)S(1)}) custom-call(bf16[256,4096]{1,0:T(8,128)(2,1)} %vec_hbm.1, bf16[256,4096]{1,0:T(8,128)(2,1)} %partner_hbm.1, bf16[32,32768]{1,0:T(8,128)(2,1)} %next_hbm.1), custom_call_target="tpu_custom_call" | custom-call | tf_op jit(solution)/shard_map/similarity/pallas_call | solution.py:311
  55.0 1.3 %finish.1 = (f32[32,256]{1,0:T(8,128)}, bf16[256,4096]{1,0:T(8,128)(2,1)}) custom-call(f32[40,256]{1,0:T(8,128)S(1)} %get-tuple-element.6.total_ref, bf16[256,4096]{1,0:T(8,128)(2,1)S(1)} %get-tuple-element.7.block_in), custom_call_target="tpu_custom_call" | custom-call | tf_op jit(solution)/shard_map/finish/pallas_call | solution.py:336

commit v4 on v3

--- a/solution.py
+++ b/solution.py
@@ -132,10 +132,14 @@
         )
 
     def next_copy(m):
-        peer = flipped(s, m, n_samp)
+        peer = flipped(s, m or n_samp - 1, n_samp)
+        first, count = {0: (next_count // 2, next_count // 2), n_samp - 1: (0, next_count // 2)}.get(
+            m, (0, next_count)
+        )
+        rows = pl.ds(first, count)
         return pltpu.make_async_remote_copy(
-            src_ref=next_hbm.at[:, pl.ds(pl.multiple_of(peer * samples, samples), samples)],
-            dst_ref=block_hbm.at[pl.ds(pl.multiple_of(s * next_count, next_count), next_count), :],
+            src_ref=next_hbm.at[rows, pl.ds(pl.multiple_of(peer * samples, samples), samples)],
+            dst_ref=block_hbm.at[pl.ds(pl.multiple_of(s * next_count + first, ALIGN), count), :],
             send_sem=next_send.at[m], recv_sem=next_recv.at[m],
             device_id=(b, peer), device_id_type=MESH,
         )
@@ -153,8 +157,9 @@
                 pair_copy(x, u).start()
 
     held = n_samp // 4
-    start_pairs(reversed(range(held, n_samp)))
-    pl.when(odd == 1)(functools.partial(start_pairs, reversed(range(held))))
+    order = [*range(n_samp - 1, 2, -1), 1, 2, 0]
+    start_pairs(order[:n_samp - held])
+    pl.when(odd == 1)(functools.partial(start_pairs, order[n_samp - held:]))
 
     @pl.when(odd == 1)
     def _():
@@ -239,6 +244,7 @@
 
     def chunk(i, carry):
         x = n_samp - 1 - i
+        x = x + jnp.where(x == 1, 1, 0) - jnp.where(x == 2, 1, 0)
         for first in range(0, samples, TREE * KTILE):
             add_unit(x, first, TREE)
         add_totals(x)
@@ -249,7 +255,8 @@
             @pl.when((x >= bit) & (x < 2 * bit))
             def _(bit=bit):
                 part_copy(x, n_samp // (2 * bit)).start()
-        pl.when((i == n_samp // 2) & (odd == 0))(functools.partial(start_pairs, reversed(range(held))))
+        pl.when(x == 1)(lambda: next_copy(0).start())
+        pl.when((i == n_samp // 2) & (odd == 0))(functools.partial(start_pairs, order[n_samp - held:]))
         return carry
 
     lax.fori_loop(0, n_samp - 1, chunk, 0)
@@ -268,7 +275,7 @@
             pair_copy(x, u).wait_send()
     for x in range(1, n_samp):
         part_copy(x, 1).wait_send()
-    for m in range(1, n_samp):
+    for m in range(n_samp):
         next_copy(m).wait()
     own_out.wait()
 
@@ -353,12 +360,12 @@
     cols = rows // n_samp
     fits = (
         n_vblk > 2
-        and n_samp > 1
+        and n_samp > 2
         and n_samp & (n_samp - 1) == 0
         and rows == ROWS_PER_DOT
         and cols % ALIGN == 0
         and samples % (TREE * KTILE) == 0
-        and next_rows.shape[0] % ALIGN == 0
+        and next_rows.shape[0] % (2 * ALIGN) == 0
         and rows * SUB * samples * 2 + 4 * rows * samples * 2 <= VMEM_BYTES
         and next_rows.shape[0] * n_samp == rows
     )

time: 56.9 us -> 56.5 us (level)
  no operation moved by 1% of the time
where the time goes in v4:
time: 56.5 us; the launch traced here: 56.3 us
  Pallas kernels  55.7 us (99%)
  between operations  0.64 us (1%)
    pallas_call x1, Pallas kernels, fused_body(): pl.pallas_call(functools.partial(kernel, n_vblk, n_samp), out_shape=(jax....  54.3 us
    pallas_call x1, Pallas kernels, fused_body(): pl.pallas_call(functools.partial(finish, groups, cols), out_shape=(jax.Sh...  1.34 us

profile of v4, /device:TPU:1, one launch (start us, length us, event | category | flops | bytes accessed | tf_op | source)
XLA Modules:
  0.0 56.3 jit_solution(17856108933992541901)
XLA Ops:
  0.6 54.3 %similarity.1 = (f32[40,256]{1,0:T(8,128)S(1)}, bf16[256,4096]{1,0:T(8,128)(2,1)S(1)}) custom-call(bf16[256,4096]{1,0:T(8,128)(2,1)} %vec_hbm.1, bf16[256,4096]{1,0:T(8,128)(2,1)} %partner_hbm.1, bf16[32,32768]{1,0:T(8,128)(2,1)} %next_hbm.1), custom_call_target="tpu_custom_call" | custom-call | tf_op jit(solution)/shard_map/similarity/pallas_call | solution.py:318
  55.0 1.3 %finish.1 = (f32[32,256]{1,0:T(8,128)}, bf16[256,4096]{1,0:T(8,128)(2,1)}) custom-call(f32[40,256]{1,0:T(8,128)S(1)} %get-tuple-element.6.total_ref, bf16[256,4096]{1,0:T(8,128)(2,1)S(1)} %get-tuple-element.7.block_in), custom_call_target="tpu_custom_call" | custom-call | tf_op jit(solution)/shard_map/finish/pallas_call | solution.py:343
